TPU v7x, 32 devices: a whole 2x2x4 slice. The times are simulated.
32 devices in a mesh: ctx: 8 (over y, x, core), tensor: 4 (over z).
Axes of the slice: x: 2, y: 2, z: 4, core: 2. Of those that a mesh axis runs over, the one named last changes fastest.
Arguments:
- queries: bfloat16 [8192, 4096], P('ctx', 'tensor'), may hold values from -6 to 6
- keys: bfloat16 [8192, 4096], P('ctx', 'tensor'), may hold values from -6 to 6
- values: bfloat16 [8192, 4096], P('ctx', 'tensor'), may hold values from -6 to 6
- doc_ids: int32 [8192], P('ctx'), may hold values from 0 to 7, never falling along the last dimension, each value on 1 to 4096 neighbouring positions
- out_weight: bfloat16 [4096, 6144], P('tensor'), may hold values from -0.125 to 0.125
- grad_out: bfloat16 [8192, 6144], P('ctx', 'tensor'), may hold values from -6 to 6
Outputs:
- attended: bfloat16 [8192, 6144], P('ctx', 'tensor')
- grad_queries: bfloat16 [8192, 4096], P('ctx', 'tensor')
- grad_keys: bfloat16 [8192, 4096], P('ctx', 'tensor')
- grad_values: bfloat16 [8192, 4096], P('ctx', 'tensor')
- grad_weight: float32 [4096, 6144], P('tensor', 'ctx')
Inputs may be any that keep to these rules, and one draw needn't show every extreme that they name: `doc_ids`: never falling along the sequence; each document has 1 to 4096 positions, and one has exactly 4096.
All inputs are finite; a program needn't handle non-finite values.
Results may differ from a plain program's by a relative error of at most 0.015.
Values may be sent and summed in bfloat16 or wider, within the bound.
A program may use at most 192 MiB of HBM per device.

v0:
```python
import jax
import jax.numpy as jnp
from jax import lax
from jax.sharding import PartitionSpec as P

HEAD = 128
careful = lax.Precision.HIGH
epsilon = 1e-06


def prefix(value, axis, combine, identity, reverse):
    length, place = (lax.axis_size(axis), lax.axis_index(axis))
    everything = jax.tree.map(
        lambda part, kind: lax.all_gather(part.astype(kind), axis),
        value,
        (jnp.bfloat16, jnp.bfloat16),
    )
    start = jax.tree.map(
        lambda part, zero: jnp.broadcast_to(jnp.asarray(zero, part.dtype), part.shape),
        value,
        identity,
    )

    def turn(k, before):
        at = length - 1 - k if reverse else k
        reached = at > place if reverse else at < place
        new = combine(
            before, jax.tree.map(lambda part, own: part[at].astype(own.dtype), everything, value)
        )
        return jax.tree.map(lambda a, b: jnp.where(reached, a, b), new, before)

    return lax.fori_loop(0, length, turn, start)


def joined_state(earlier, later):
    earlier_doc, earlier_state = earlier
    later_doc, later_state = later
    vacant = later_doc < 0
    keeping = (earlier_doc == later_doc) | vacant
    doc_result = jnp.where(vacant, earlier_doc, later_doc)
    state_result = later_state + jnp.where(keeping, earlier_state, jnp.zeros_like(earlier_state))
    return (doc_result, state_result)


def carried(doc_cell, state, backward):
    identity = (jnp.full((1, 1, 1), -1.0, jnp.float32), jnp.zeros_like(state))
    if backward:
        doc_in, state_in = prefix((doc_cell, state), "ctx", joined_state, identity, True)
    else:
        doc_in, state_in = prefix((doc_cell, state), "ctx", joined_state, identity, False)
    return (doc_in.reshape(()), state_in)


def body(queries, keys, values, doc_ids, out_weight, grad_out):
    rows = queries.shape[0]
    head_size = HEAD
    heads_here = queries.shape[1] // head_size
    query_rows = queries.reshape(rows, heads_here, head_size)
    key_rows = keys.reshape(rows, heads_here, head_size)
    value_rows = values.reshape(rows, heads_here, head_size)
    doc_float = doc_ids.astype(jnp.float32)
    order = jnp.arange(rows)
    mask = ((order[:, None] >= order[None, :]) & (doc_float[:, None] == doc_float[None, :])).astype(
        jnp.float32
    )
    scores = (
        jnp.einsum("the,uhe->htu", query_rows, key_rows, preferred_element_type=jnp.float32)
        * mask[None]
    )
    local = jnp.einsum(
        "htu,uhf->thf", scores, value_rows, precision=careful, preferred_element_type=jnp.float32
    )
    tail_mask = (doc_float == doc_float[-1]).astype(jnp.bfloat16)[:, None, None]
    tail_state = jnp.einsum(
        "uhe,uhf->hef", key_rows * tail_mask, value_rows, preferred_element_type=jnp.float32
    )
    last_doc, state_in = carried(doc_float[-1].reshape(1, 1, 1), tail_state, False)
    joined = (doc_float == last_doc).astype(jnp.float32)[:, None, None]
    opened = local + joined * jnp.einsum(
        "the,hef->thf", query_rows, state_in, precision=careful, preferred_element_type=jnp.float32
    )
    inverse = lax.rsqrt(jnp.mean(opened * opened, axis=-1, keepdims=True) + epsilon)
    normed = opened * inverse
    normed_low = normed.reshape(rows, heads_here * head_size).astype(jnp.bfloat16)
    partial_out = jnp.dot(normed_low, out_weight, preferred_element_type=jnp.float32)
    attended = lax.psum_scatter(
        partial_out.astype(jnp.bfloat16), "tensor", scatter_dimension=1, tiled=True
    )
    grad_whole = lax.all_gather(grad_out, "tensor", axis=1, tiled=True)
    grad_normed = lax.dot_general(
        grad_whole, out_weight, (((1,), (1,)), ((), ())), preferred_element_type=jnp.float32
    )
    weight_term = lax.dot_general(
        normed_low, grad_whole, (((0,), (0,)), ((), ())), preferred_element_type=jnp.float32
    )
    grad_weight = lax.psum_scatter(
        weight_term.astype(jnp.bfloat16), "ctx", scatter_dimension=1, tiled=True
    ).astype(jnp.float32)
    grad_normed = grad_normed.reshape(rows, heads_here, head_size)
    grad_opened = inverse * (
        grad_normed - normed * jnp.mean(grad_normed * normed, axis=-1, keepdims=True)
    )
    head_mask = (doc_float == doc_float[0]).astype(jnp.bfloat16)[:, None, None]
    head_state = jnp.einsum(
        "the,thf->hef",
        query_rows * head_mask,
        grad_opened,
        precision=careful,
        preferred_element_type=jnp.float32,
    )
    first_doc, state_back = carried(doc_float[0].reshape(1, 1, 1), head_state, True)
    starts = (doc_float == first_doc).astype(jnp.float32)[:, None, None]
    grad_scores = (
        jnp.einsum(
            "thf,uhf->htu",
            grad_opened,
            value_rows,
            precision=careful,
            preferred_element_type=jnp.float32,
        )
        * mask[None]
    )
    grad_query = jnp.einsum(
        "htu,uhe->the", grad_scores, key_rows, precision=careful, preferred_element_type=jnp.float32
    ) + joined * jnp.einsum(
        "thf,hef->the", grad_opened, state_in, precision=careful, preferred_element_type=jnp.float32
    )
    grad_key = jnp.einsum(
        "htu,the->uhe",
        grad_scores,
        query_rows,
        precision=careful,
        preferred_element_type=jnp.float32,
    ) + starts * jnp.einsum(
        "uhf,hef->uhe",
        value_rows,
        state_back,
        precision=careful,
        preferred_element_type=jnp.float32,
    )
    grad_value = jnp.einsum(
        "htu,thf->uhf", scores, grad_opened, precision=careful, preferred_element_type=jnp.float32
    ) + starts * jnp.einsum(
        "uhe,hef->uhf", key_rows, state_back, precision=careful, preferred_element_type=jnp.float32
    )
    flat = heads_here * head_size
    return (
        attended,
        grad_query.reshape(rows, flat).astype(jnp.bfloat16),
        grad_key.reshape(rows, flat).astype(jnp.bfloat16),
        grad_value.reshape(rows, flat).astype(jnp.bfloat16),
        grad_weight,
    )


def solution(mesh):
    return jax.shard_map(
        body,
        mesh=mesh,
        in_specs=(
            P("ctx", "tensor"),
            P("ctx", "tensor"),
            P("ctx", "tensor"),
            P("ctx"),
            P("tensor", None),
            P("ctx", "tensor"),
        ),
        out_specs=(
            P("ctx", "tensor"),
            P("ctx", "tensor"),
            P("ctx", "tensor"),
            P("ctx", "tensor"),
            P("tensor", "ctx"),
        ),
        check_vma=False,
    )
```

profile of v0, /device:TPU:0, one launch (start us, length us, event | category | flops | bytes accessed | tf_op | source)
XLA Modules:
  0.0 642.6 jit_solution(15173689273183936138)
XLA Ops:
  8.6 3.6 copy.65
  12.2 4.1 copy.36
  16.3 1.3 compare_convert_fusion.1
  17.6 3.1 fusion.46
  22.7 1.4 dynamic-update-slice
  24.1 1.4 dynamic-update-slice.1
  25.5 15.8 %all-reduce.2 = (bf16[8]{0:T(256)(128)(2,1)S(1)}, bf16[8]{0:T(256)(128)(2,1)}) all-reduce(bf16[8]{0:T(256)(128)(2,1)S(1)} %dynamic-update-slice, bf16[8]{0:T(256)(128)(2,1)S(1)} %dynamic-update-slice.1), channel_id=2, replica_groups=mesh['ctx'=8,'tensor'=4] {'ctx'}, use_global_device_ids=true, to_apply=%add | all-reduce | flops 16 | bytes 64
  41.3 4.0 copy.62
  45.3 2.8 fusion.17
  49.1 14.8 %fusion.32 = f32[8,1024,1024]{2,1,0:T(8,128)} fusion(bf16[1024,8,128]{0,2,1:T(8,128)(2,1)S(1)} %bitcast.128, bf16[1024,1024]{1,0:T(8,128)(2,1)S(1)} %copy-done.7), kind=kOutput, calls=%fused_computation.41 | convolution fusion | flops 2147483648 | bytes 37748736 | tf_op jit(solution)/shard_map/the,uhe->htu/dot_general | solution.py:67
  63.9 31.0 %while.34 = (s32[]{:T(128)}, f32[1,1,1]{2,1,0:T(1,128)}, f32[8,128,128]{2,1,0:T(8,128)S(1)}, s32[]{:T(128)}, bf16[8,1,1,1]{0,3,2,1:T(2,128)(2,1)S(1)}, /*index=5...) while((s32[]{:T(128)}, f32[1,1,1]{2,1,0:T(1,128)}, ...), condition=%wide.region_1.2_spmd.clone, body=%wide.region_0.1_spmd.clone.sunk | while | flops 655369 | bytes 1310887 | solution.py:32
  65.8 1.3 fusion.83
  69.7 1.3 fusion.83
  73.6 1.3 fusion.83
  77.5 1.3 fusion.83
  81.4 1.3 fusion.83
  89.1 1.3 fusion.83
  93.0 1.3 fusion.83
  94.9 4.9 fusion.55
  99.8 21.0 %multiply_reduce_fusion.1 = (f32[1024,8]{0,1:T(8,128)S(1)}, f32[1024,8,128]{0,2,1:T(8,128)}) fusion(f32[8,128,1024]{2,1,0:T(8,128)} %fusion.55, f32[1024]{0:T(1024)S(1)} %compare_convert_fusion.2, f32[8,1024,1024]{2,1,0:T(8,128)} %fusion.32, f32[1024,1024]{1,0:T(8,128)} %fusion.17, bf16[1024,1024]{1,0:T(8,128)(2,1)S(1)} %copy-done), kind=kOutput, calls=%fused_computation.28 | convolution fusion | flops 6455025664 | bytes 48271360 | tf_op jit(solution)/shard_map/htu,uhf->thf/dot_general | solution.py:70
  120.8 150.5 %all-gather.8.cloned.1.call-done = bf16[1024,6144]{1,0:T(8,128)(2,1)} async-done(((bf16[1024,1536]{1,0:T(8,128)(2,1)}), bf16[1024,6144]{1,0:T(8,128)(2,1)}) %all-gather.8.cloned.1.call-update) | async-done | bytes 12582928 | tf_op jit(solution)/shard_map/all_gather | solution.py:89
  271.3 21.3 %multiply_reduce_fusion = (f32[1024,8]{0,1:T(8,128)S(1)}, f32[1024,1024]{0,1:T(8,128)S(1)}) fusion(f32[1024,8,128]{0,2,1:T(8,128)} %get-tuple-element.385, f32[1024,8]{0,1:T(8,128)S(1)} %add_rsqrt_fusion, bf16[1024,6144]{1,0:T(8,128)(2,1)} %all-gather.8.cloned.1.call-done, bf16[1024,6144]{1,0:T(8,128)(2,1)} %param.14), kind=kOutput, calls=%fused_computation.27 | convolution fusion | flops 12888039424 | bytes 33619968 | tf_op jit(solution)/shard_map/dot_general | solution.py:90
  292.7 3.0 subtract_multiply_fusion
  295.6 2.0 copy-done.3
  297.6 2.1 fusion.43
  299.7 20.9 %convolution_convert_fusion = bf16[1024,6144]{1,0:T(8,128)(2,1)} fusion(bf16[1024,1024]{0,1:T(8,128)(2,1)} %bitcast.136, bf16[1024,6144]{1,0:T(8,128)(2,1)} %all-gather.8.cloned.1.call-done), kind=kOutput, calls=%fused_computation.18 | convolution fusion | flops 12891193344 | bytes 27262976 | tf_op jit(solution)/shard_map/dot_general | solution.py:93
  320.7 22.6 %convolution_convert_fusion.1 = bf16[1024,6144]{1,0:T(8,128)(2,1)} fusion(bf16[1024,1024]{0,1:T(8,128)(2,1)} %bitcast.137, bf16[1024,6144]{1,0:T(8,128)(2,1)} %param.14), kind=kOutput, calls=%fused_computation.19 | convolution fusion | flops 12891193344 | bytes 27262976 | tf_op jit(solution)/shard_map/dot_general | solution.py:85
  343.4 7.2 %fusion.56 = f32[8,128,1024]{2,1,0:T(8,128)} fusion(f32[8,128,128]{2,1,0:T(8,128)S(1)} %get-tuple-element.271, f32[1024,8,128]{0,2,1:T(8,128)} %copy-done.3), kind=kOutput, calls=%fused_computation.67 | convolution fusion | flops 805306368 | bytes 8912896 | tf_op jit(solution)/shard_map/thf,hef->the/dot_general | solution.py:125
  350.6 18.5 %fusion.27 = f32[8,1024,1024]{2,1,0:T(8,128)} fusion(f32[1024,8,128]{0,2,1:T(8,128)} %copy-done.3, bf16[1024,1024]{1,0:T(8,128)(2,1)S(1)} %copy-done), kind=kOutput, calls=%fused_computation.36 | convolution fusion | flops 6442450944 | bytes 39845888 | tf_op jit(solution)/shard_map/thf,uhf->htu/dot_general | solution.py:114
  369.2 19.0 %fusion.15 = bf16[1024,8,128]{0,2,1:T(8,128)(2,1)} fusion(f32[8,128,1024]{2,1,0:T(8,128)} %fusion.56, bf16[1024,8,128]{0,2,1:T(8,128)(2,1)} %copy.36, f32[8,1024,1024]{2,1,0:T(8,128)} %fusion.27, f32[1024,1024]{1,0:T(8,128)S(1)} %copy-done.1, f32[1024]{0:T(1024)S(1)} %compare_convert_fusion.2), kind=kOutput, calls=%fused_computation.23 | convolution fusion | flops 6453985280 | bytes 46141440 | tf_op jit(solution)/shard_map/htu,uhe->the/dot_general | solution.py:123
  388.1 3.9 copy.52
  392.1 19.4 %fusion.6 = f32[8,128,1024]{2,1,0:T(8,128)} fusion(f32[1024,8,128]{0,2,1:T(8,128)} %copy-done.3, f32[8,1024,1024]{2,1,0:T(8,128)} %fusion.32, f32[1024,1024]{1,0:T(8,128)} %fusion.17), kind=kOutput, calls=%fused_computation.10 | convolution fusion | flops 6450839552 | bytes 46137344 | tf_op jit(solution)/shard_map/htu,thf->uhf/dot_general | solution.py:141
  411.4 31.1 %while.35 = (s32[]{:T(128)}, f32[1,1,1]{2,1,0:T(1,128)}, f32[8,128,128]{2,1,0:T(8,128)S(1)}, s32[]{:T(128)}, bf16[8,1,1,1]{0,3,2,1:T(2,128)(2,1)S(1)}, /*index=5...) while((s32[]{:T(128)}, f32[1,1,1]{2,1,0:T(1,128)}, ...), condition=%wide.region_6.7_spmd.clone, body=%wide.region_5.6_spmd.clone.sunk | while | flops 655373 | bytes 1310949 | solution.py:32
  413.4 1.3 fusion.84
  417.2 1.3 fusion.84
  421.1 1.3 fusion.84
  424.9 1.3 fusion.84
  428.8 1.3 fusion.84
  432.7 1.3 fusion.84
  436.6 1.3 fusion.84
  440.4 1.3 fusion.84
  442.5 5.7 add_convert_fusion
  448.2 3.9 copy.54
  452.2 1.3 fusion.25
  455.0 17.1 %fusion.14 = bf16[1024,8,128]{0,2,1:T(8,128)(2,1)} fusion(f32[8,128,1024]{2,1,0:T(8,128)S(1)} %fusion.25, bf16[1024,8,128]{0,2,1:T(8,128)(2,1)S(1)} %bitcast.130, f32[8,1024,1024]{2,1,0:T(8,128)} %fusion.27, f32[1024,1024]{1,0:T(8,128)S(1)} %copy-done.2, f32[1024]{0:T(1024)S(1)} %compare_convert_fusion), kind=kOutput, calls=%fused_computation.21 | convolution fusion | flops 6453985280 | bytes 46141440 | tf_op jit(solution)/shard_map/htu,the->uhe/dot_general | solution.py:128
  472.1 4.0 copy.53
  476.1 3.3 convert_element_type.139
  479.4 156.5 %reduce-scatter.3.cloned.1.call-done = bf16[1024,1536]{1,0:T(8,128)(2,1)} async-done(((bf16[1024,6144]{1,0:T(8,128)(2,1)}), bf16[1024,1536]{1,0:T(8,128)(2,1)}) %reduce-scatter.3.cloned.1.call-update) | async-done | bytes 3145744 | tf_op jit(solution)/shard_map/reduce_scatter | solution.py:86
  (69 shorter events, 17.4 us)
Async XLA Ops:
  7.2 10.4 %copy-start = (bf16[1024,1024]{1,0:T(8,128)(2,1)S(1)}, bf16[1024,1024]{1,0:T(8,128)(2,1)}, u32[]{:S(2)}) copy-start(bf16[1024,1024]{1,0:T(8,128)(2,1)} %param.12) | copy-start | bytes 6291460
  7.2 56.7 %all-gather.10.cloned.1.call-start = ((), (), s32[]{:S(2)}) async-start(), calls=%async_computation.5 | async-start | bytes 2359296 | tf_op jit(solution)/shard_map/all_gather | solution.py:14
  8.6 7.7 %copy-start.10 = (s32[1024]{0:T(1024)S(1)}, s32[1024]{0:T(1024)}, u32[]{:S(2)}) copy-start(s32[1024]{0:T(1024)} %param.13) | copy-start | bytes 12292
  17.6 3.9 copy-start.13
  20.7 250.5 %all-gather.8.cloned.1.call-start = ((), (), s32[]{:S(2)}) async-start(), calls=%async_computation.3 | async-start | bytes 15728640 | tf_op jit(solution)/shard_map/all_gather | solution.py:89
  21.5 389.9 %all-gather.12.cloned.1.call-start = ((), (), s32[]{:S(2)}) async-start(), calls=%async_computation.6 | async-start | bytes 2359296 | tf_op jit(solution)/shard_map/all_gather | solution.py:14
  45.3 2.8 copy-start.4
  45.3 3.8 copy-start.7
  271.3 21.3 %copy-start.8 = (f32[1024,8,128]{0,2,1:T(8,128)S(1)}, f32[1024,8,128]{0,2,1:T(8,128)}, u32[]{:S(2)}) copy-start(f32[1024,8,128]{0,2,1:T(8,128)} %get-tuple-element.385) | copy-start | bytes 12582916
  292.6 5.0 copy-start.5
  295.6 2.0 copy-start.3
  299.7 176.4 %reduce-scatter.5.cloned.1.call-start = ((), (), s32[]{:S(2)}) async-start(), calls=%async_computation.4 | async-start | bytes 14155776 | tf_op jit(solution)/shard_map/reduce_scatter | solution.py:96
  320.7 315.2 %reduce-scatter.3.cloned.1.call-start = ((), (), s32[]{:S(2)}) async-start(), calls=%async_computation.2 | async-start | bytes 15728640 | tf_op jit(solution)/shard_map/reduce_scatter | solution.py:86
  350.6 18.5 %copy-start.1 = (f32[1024,1024]{1,0:T(8,128)S(1)}, f32[1024,1024]{1,0:T(8,128)}, u32[]{:S(2)}) copy-start(f32[1024,1024]{1,0:T(8,128)} %fusion.17) | copy-start | bytes 12582916
  392.1 19.4 %copy-start.9 = (f32[8,128,128]{2,1,0:T(8,128)S(1)}, f32[8,128,128]{2,1,0:T(8,128)}, u32[]{:S(2)}) copy-start(f32[8,128,128]{2,1,0:T(8,128)} %custom-call.1) | copy-start | bytes 1572868
  392.1 19.4 %copy-start.12 = (bf16[8]{0:T(256)(128)(2,1)S(1)}, bf16[8]{0:T(256)(128)(2,1)}, u32[]{:S(2)}) copy-start(bf16[8]{0:T(256)(128)(2,1)} %get-tuple-element.375) | copy-start | bytes 52
  411.4 31.1 %copy-start.11 = (s32[1024]{0:T(1024)S(1)}, s32[1024]{0:T(1024)}, u32[]{:S(2)}) copy-start(s32[1024]{0:T(1024)} %param.13) | copy-start | bytes 12292
  452.2 2.2 copy-start.2
  452.2 2.9 copy-start.6
Sparse Core Ops, SparseCore 0:
  20.9 30.5 all-gather.9
  53.1 218.1 all-gather.7
  299.8 25.9 all-gather.11
  329.2 91.9 reduce-scatter.4
  423.9 211.8 reduce-scatter.2
where the time goes:
time: 652 us; the launch traced here: 643 us
  waiting for transfers between devices  308 us (47%)
  matrix products  199 us (31%)
  local copies, waits for them, and re-layouts  42.5 us (7%)
  loops' own time  31.9 us (5%)
  other arithmetic  31.5 us (5%)
  blocking collectives  15.8 us (2%)
  between operations  14.1 us (2%)
    reduce_scatter x1, waiting for transfers between devices, body(): lax.psum_scatter(partial_out.astype(jnp.bfloat16), 'tensor', scatter_dime...  156 us
    all_gather x1, waiting for transfers between devices, body(): grad_whole = lax.all_gather(grad_out, 'tensor', axis=1, tiled=True)  150 us
    another operation x2, loops' own time, prefix(): return lax.fori_loop(0, length, turn, start)  31.9 us
    unnamed x37, local copies, waits for them, and re-layouts  23.4 us
    dot_general x1, matrix products, body(): jnp.dot(normed_low, out_weight, preferred_element_type=jnp.float32)  22.6 us
    dot_general x1, matrix products, body(): lax.dot_general(grad_whole, out_weight, (((1,), (1,)), ((), ())), preferr...  21.3 us
    dot_general x1, matrix products, body(): jnp.einsum('htu,uhf->thf', scores, value_rows, precision=careful, preferr...  21 us
    dot_general x1, matrix products, body(): lax.dot_general(normed_low, grad_whole, (((0,), (0,)), ((), ())), preferr...  20.9 us
  transfers between devices with their start and end apart: 5, of which 2 were waited for; matrix products, arithmetic and copies ran while one was open for 36% of the time, Pallas kernels for 0%

commit v1 on v0

--- a/solution.py
+++ b/solution.py
@@ -86,7 +86,14 @@
     attended = lax.psum_scatter(
         partial_out.astype(jnp.bfloat16), "tensor", scatter_dimension=1, tiled=True
     )
-    grad_whole = lax.all_gather(grad_out, "tensor", axis=1, tiled=True)
+    ring = [grad_out]
+    for hop in range(3):
+        ring.append(lax.ppermute(ring[-1], "tensor", [(dev, (dev + 1) % 4) for dev in range(4)]))
+    grad_whole = jnp.roll(
+        jnp.concatenate(ring[::-1], axis=1),
+        (lax.axis_index("tensor") + 1) * ring[0].shape[1],
+        axis=1,
+    )
     grad_normed = lax.dot_general(
         grad_whole, out_weight, (((1,), (1,)), ((), ())), preferred_element_type=jnp.float32
     )

time: 652 us -> 627 us (0.962)
  waiting for transfers between devices: 308 us -> 258 us
  local copies, waits for them, and re-layouts: 42.5 us -> 69.2 us
    all_gather x1 -> x0, waiting for transfers between devices: 150 us -> none  [body(): grad_whole = lax.all_gather(grad_out, 'tensor', axis=1, tiled=True)]
    ppermute x0 -> x3, waiting for transfers between devices: none -> 102 us  [body(): lax.ppermute(ring[-1], 'tensor', [(dev, (dev + 1) % 4) for dev in range(4)])]
    unnamed x37 -> x42, local copies, waits for them, and re-layouts: 23.4 us -> 48.6 us
  transfers between devices with their start and end apart: 5 -> 7, of which waited for: 2 -> 4; matrix products, arithmetic and copies ran while one was open for 36% -> 39% of each run, Pallas kernels for 0% -> 0%
where the time goes in v1:
time: 627 us; the launch traced here: 619 us
  waiting for transfers between devices  258 us (41%)
  matrix products  199 us (32%)
  local copies, waits for them, and re-layouts  69.2 us (11%)
  other arithmetic  30.8 us (5%)
  loops' own time  30 us (5%)
  blocking collectives  14.3 us (2%)
  between operations  14.2 us (2%)
    reduce_scatter x1, waiting for transfers between devices, body(): lax.psum_scatter(partial_out.astype(jnp.bfloat16), 'tensor', scatter_dime...  156 us
    ppermute x3, waiting for transfers between devices, body(): lax.ppermute(ring[-1], 'tensor', [(dev, (dev + 1) % 4) for dev in range(4)])  102 us
    unnamed x42, local copies, waits for them, and re-layouts  48.6 us
    another operation x2, loops' own time, prefix(): return lax.fori_loop(0, length, turn, start)  30 us
    dot_general x1, matrix products, body(): jnp.dot(normed_low, out_weight, preferred_element_type=jnp.float32)  22.8 us
    dot_general x1, matrix products, body(): lax.dot_general(normed_low, grad_whole, (((0,), (0,)), ((), ())), preferr...  21.3 us
    dot_general x1, matrix products, body(): jnp.einsum('htu,uhf->thf', scores, value_rows, precision=careful, preferr...  20.9 us
    select_n x16, other arithmetic, turn(): return jax.tree.map(lambda a, b: jnp.where(reached, a, b), new, before)  20.4 us
  transfers between devices with their start and end apart: 7, of which 4 were waited for; matrix products, arithmetic and copies ran while one was open for 39% of the time, Pallas kernels for 0%

profile of v1, /device:TPU:0, one launch (start us, length us, event | category | flops | bytes accessed | tf_op | source)
XLA Modules:
  0.0 618.7 jit_solution(11062554896783065377)
XLA Ops:
  7.2 3.1 collective-permute-start
  11.0 3.6 copy.65
  14.6 4.1 copy.36
  19.3 1.3 compare_convert_fusion.1
  20.6 3.1 fusion.49
  23.8 3.9 copy.62
  28.9 1.4 dynamic-update-slice.1
  30.4 1.4 dynamic-update-slice
  31.8 49.0 %collective-permute-done = bf16[1024,1536]{1,0:T(8,128)(2,1)} collective-permute-done((bf16[1024,1536]{1,0:T(8,128)(2,1)}, bf16[1024,1536]{1,0:T(8,128)(2,1)}, u32[]{:S(2)}, u32[]{:S(2)}) %collective-permute-start) | collective-permute-done | bytes 3145760 | tf_op jit(solution)/shard_map/ppermute | solution.py:91
  80.8 17.8 %fusion.35 = f32[8,1024,1024]{2,1,0:T(8,128)} fusion(bf16[1024,8,128]{0,2,1:T(8,128)(2,1)} %bitcast.125, bf16[1024,1024]{1,0:T(8,128)(2,1)} %param.11), kind=kOutput, calls=%fused_computation.44 | convolution fusion | flops 2147483648 | bytes 37748736 | tf_op jit(solution)/shard_map/the,uhe->htu/dot_general | solution.py:67
  98.6 14.3 %all-reduce.2 = (bf16[8]{0:T(256)(128)(2,1)S(1)}, bf16[8]{0:T(256)(128)(2,1)}) all-reduce(bf16[8]{0:T(256)(128)(2,1)S(1)} %dynamic-update-slice, bf16[8]{0:T(256)(128)(2,1)S(1)} %dynamic-update-slice.1), channel_id=2, replica_groups=mesh['ctx'=8,'tensor'=4] {'ctx'}, use_global_device_ids=true, to_apply=%add | all-reduce | flops 16 | bytes 64
  112.9 2.6 fusion.20
  115.5 28.7 %while.34 = (s32[]{:T(128)}, f32[1,1,1]{2,1,0:T(1,128)}, f32[8,128,128]{2,1,0:T(8,128)S(1)}, s32[]{:T(128)}, bf16[8,1,1,1]{0,3,2,1:T(2,128)(2,1)S(1)}, /*index=5...) while((s32[]{:T(128)}, f32[1,1,1]{2,1,0:T(1,128)}, ...), condition=%wide.region_1.2_spmd.clone, body=%wide.region_0.1_spmd.clone.sunk | while | flops 655369 | bytes 1310895 | solution.py:32
  117.8 1.3 fusion.86
  121.3 1.3 fusion.86
  144.2 8.0 %collective-permute-done.1 = bf16[1024,1536]{1,0:T(8,128)(2,1)} collective-permute-done((bf16[1024,1536]{1,0:T(8,128)(2,1)}, bf16[1024,1536]{1,0:T(8,128)(2,1)}, u32[]{:S(2)}, u32[]{:S(2)}) %collective-permute-start.1) | collective-permute-done | bytes 3145760 | tf_op jit(solution)/shard_map/ppermute | solution.py:91
  152.3 4.8 fusion.60
  157.2 20.9 %multiply_reduce_fusion.1 = (f32[1024,8]{0,1:T(8,128)S(1)}, f32[1024,8,128]{0,2,1:T(8,128)}) fusion(f32[8,128,1024]{2,1,0:T(8,128)} %fusion.60, f32[1024]{0:T(1024)S(1)} %compare_convert_fusion.2, f32[8,1024,1024]{2,1,0:T(8,128)} %fusion.35, f32[1024,1024]{1,0:T(8,128)} %fusion.20, bf16[1024,1024]{1,0:T(8,128)(2,1)S(1)} %copy-done), kind=kOutput, calls=%fused_computation.31 | convolution fusion | flops 6455025664 | bytes 48271360 | tf_op jit(solution)/shard_map/htu,uhf->thf/dot_general | solution.py:70
  178.1 44.8 %collective-permute-done.2 = bf16[1024,1536]{1,0:T(8,128)(2,1)} collective-permute-done((bf16[1024,1536]{1,0:T(8,128)(2,1)}, bf16[1024,1536]{1,0:T(8,128)(2,1)}, u32[]{:S(2)}, u32[]{:S(2)}) %collective-permute-start.2) | collective-permute-done | bytes 3145760 | tf_op jit(solution)/shard_map/ppermute | solution.py:91
  222.8 3.8 constant_dynamic-update-slice_fusion.7
  226.6 3.8 constant_dynamic-update-slice_fusion.6
  230.4 3.9 constant_dynamic-update-slice_fusion.5
  234.3 1.9 constant_dynamic-update-slice_fusion.4
  236.3 3.8 constant_dynamic-update-slice_fusion.3
  240.0 3.8 constant_dynamic-update-slice_fusion.2
  243.8 3.7 constant_dynamic-update-slice_fusion.1
  247.6 1.9 constant_dynamic-update-slice_fusion
  249.5 1.4 copy-done.6
  250.9 18.5 %multiply_reduce_fusion = (f32[1024,8]{0,1:T(8,128)S(1)}, f32[1024,1024]{0,1:T(8,128)S(1)}) fusion(f32[1024,8,128]{0,2,1:T(8,128)S(1)} %copy-done.6, f32[1024,8]{0,1:T(8,128)S(1)} %add_rsqrt_fusion, bf16[1024,6144]{1,0:T(8,128)(2,1)} %param.14, bf16[1024,12288]{1,0:T(8,128)(2,1)} %constant_dynamic-update-slice_fusion, s32[]{:T(128)S(6)} %select_n.132), kind=kOutput, calls=%fused_computation.30 | convolution fusion | flops 12888039424 | bytes 33619972 | tf_op jit(solution)/shard_map/dot_general | solution.py:97
  269.4 2.6 subtract_multiply_fusion
  272.0 2.0 copy-done.3
  273.9 2.1 fusion.46
  276.1 21.3 %convolution_convert_fusion = bf16[1024,6144]{1,0:T(8,128)(2,1)} fusion(bf16[1024,1024]{0,1:T(8,128)(2,1)} %bitcast.134, bf16[1024,12288]{1,0:T(8,128)(2,1)} %constant_dynamic-update-slice_fusion, s32[]{:T(128)S(6)} %select_n.132), kind=kOutput, calls=%fused_computation.18 | convolution fusion | flops 12891193344 | bytes 27262980 | tf_op jit(solution)/shard_map/dot_general | solution.py:100
  297.5 22.8 %convolution_convert_fusion.1 = bf16[1024,6144]{1,0:T(8,128)(2,1)} fusion(bf16[1024,1024]{0,1:T(8,128)(2,1)} %bitcast.135, bf16[1024,6144]{1,0:T(8,128)(2,1)} %param.14), kind=kOutput, calls=%fused_computation.19 | convolution fusion | flops 12891193344 | bytes 27262976 | tf_op jit(solution)/shard_map/dot_general | solution.py:85
  320.3 7.2 %fusion.61 = f32[8,128,1024]{2,1,0:T(8,128)} fusion(f32[8,128,128]{2,1,0:T(8,128)S(1)} %get-tuple-element.271, f32[1024,8,128]{0,2,1:T(8,128)} %copy-done.3), kind=kOutput, calls=%fused_computation.80 | convolution fusion | flops 805306368 | bytes 8912896 | tf_op jit(solution)/shard_map/thf,hef->the/dot_general | solution.py:132
  327.5 18.3 %fusion.30 = f32[8,1024,1024]{2,1,0:T(8,128)} fusion(f32[1024,8,128]{0,2,1:T(8,128)} %copy-done.3, bf16[1024,1024]{1,0:T(8,128)(2,1)S(1)} %copy-done), kind=kOutput, calls=%fused_computation.39 | convolution fusion | flops 6442450944 | bytes 39845888 | tf_op jit(solution)/shard_map/thf,uhf->htu/dot_general | solution.py:121
  345.8 18.8 %fusion.18 = bf16[1024,8,128]{0,2,1:T(8,128)(2,1)} fusion(f32[8,128,1024]{2,1,0:T(8,128)} %fusion.61, bf16[1024,8,128]{0,2,1:T(8,128)(2,1)} %copy.36, f32[8,1024,1024]{2,1,0:T(8,128)} %fusion.30, f32[1024,1024]{1,0:T(8,128)S(1)} %copy-done.1, f32[1024]{0:T(1024)S(1)} %compare_convert_fusion.2), kind=kOutput, calls=%fused_computation.26 | convolution fusion | flops 6453985280 | bytes 46141440 | tf_op jit(solution)/shard_map/htu,uhe->the/dot_general | solution.py:130
  364.6 3.9 copy.52
  368.5 19.0 %fusion.6 = f32[8,128,1024]{2,1,0:T(8,128)} fusion(f32[1024,8,128]{0,2,1:T(8,128)} %copy-done.3, f32[8,1024,1024]{2,1,0:T(8,128)} %fusion.35, f32[1024,1024]{1,0:T(8,128)} %fusion.20), kind=kOutput, calls=%fused_computation.10 | convolution fusion | flops 6450839552 | bytes 46137344 | tf_op jit(solution)/shard_map/htu,thf->uhf/dot_general | solution.py:148
  387.6 31.1 %while.35 = (s32[]{:T(128)}, f32[1,1,1]{2,1,0:T(1,128)}, f32[8,128,128]{2,1,0:T(8,128)S(1)}, s32[]{:T(128)}, bf16[8,1,1,1]{0,3,2,1:T(2,128)(2,1)S(1)}, /*index=5...) while((s32[]{:T(128)}, f32[1,1,1]{2,1,0:T(1,128)}, ...), condition=%wide.region_6.7_spmd.clone, body=%wide.region_5.6_spmd.clone.sunk | while | flops 655373 | bytes 1310957 | solution.py:32
  405.6 1.3 fusion.87
  418.7 5.7 add_convert_fusion
  424.4 3.9 copy.54
  428.3 1.3 fusion.28
  431.2 17.1 %fusion.17 = bf16[1024,8,128]{0,2,1:T(8,128)(2,1)} fusion(f32[8,128,1024]{2,1,0:T(8,128)S(1)} %fusion.28, bf16[1024,8,128]{0,2,1:T(8,128)(2,1)S(1)} %bitcast.128, f32[8,1024,1024]{2,1,0:T(8,128)} %fusion.30, f32[1024,1024]{1,0:T(8,128)S(1)} %copy-done.2, f32[1024]{0:T(1024)S(1)} %compare_convert_fusion), kind=kOutput, calls=%fused_computation.24 | convolution fusion | flops 6453985280 | bytes 46141440 | tf_op jit(solution)/shard_map/htu,the->uhe/dot_general | solution.py:135
  448.3 4.0 copy.53
  452.2 3.3 convert_element_type.139
  455.5 156.4 %reduce-scatter.3.cloned.1.call-done = bf16[1024,1536]{1,0:T(8,128)(2,1)} async-done(((bf16[1024,6144]{1,0:T(8,128)(2,1)}), bf16[1024,1536]{1,0:T(8,128)(2,1)}) %reduce-scatter.3.cloned.1.call-update) | async-done | bytes 3145744 | tf_op jit(solution)/shard_map/reduce_scatter | solution.py:86
  (78 shorter events, 30.4 us)
Async XLA Ops:
  7.2 13.4 %copy-start = (bf16[1024,1024]{1,0:T(8,128)(2,1)S(1)}, bf16[1024,1024]{1,0:T(8,128)(2,1)}, u32[]{:S(2)}) copy-start(bf16[1024,1024]{1,0:T(8,128)(2,1)} %param.12) | copy-start | bytes 6291460
  7.2 108.3 %all-gather.7.cloned.1.call-start = ((), (), s32[]{:S(2)}) async-start(), calls=%async_computation.4 | async-start | bytes 2359296 | tf_op jit(solution)/shard_map/all_gather | solution.py:14
  7.2 73.5 %collective-permute-start = (bf16[1024,1536]{1,0:T(8,128)(2,1)}, bf16[1024,1536]{1,0:T(8,128)(2,1)}, u32[]{:S(2)}, u32[]{:S(2)}) collective-permute-start(bf16[1024,1536]{1,0:T(8,128)(2,1)} %param.15), channel_id=1, source_target_pairs={{0,1},{1,2},{2,3},{3,0},{4,5},{5,6},{6,7},{7,4},{8,9},{9,10},{10,1... | collective-permute-start | bytes 9437192 | tf_op jit(solution)/shard_map/ppermute | solution.py:91
  11.0 8.2 %copy-start.9 = (s32[1024]{0:T(1024)S(1)}, s32[1024]{0:T(1024)}, u32[]{:S(2)}) copy-start(s32[1024]{0:T(1024)} %param.13) | copy-start | bytes 12292
  20.6 7.1 %copy-start.12 = (u32[32]{0:T(128)S(1)}, u32[32]{0:T(128)}, u32[]{:S(2)}) copy-start(u32[32]{0:T(128)} %constant.140) | copy-start | bytes 388
  23.7 363.9 %all-gather.9.cloned.1.call-start = ((), (), s32[]{:S(2)}) async-start(), calls=%async_computation.5 | async-start | bytes 2359296 | tf_op jit(solution)/shard_map/all_gather | solution.py:14
  80.8 71.4 %collective-permute-start.1 = (bf16[1024,1536]{1,0:T(8,128)(2,1)}, bf16[1024,1536]{1,0:T(8,128)(2,1)}, u32[]{:S(2)}, u32[]{:S(2)}) collective-permute-start(bf16[1024,1536]{1,0:T(8,128)(2,1)} %collective-permute-done), channel_id=1, source_target_pairs={{0,1},{1,2},{2,3},{3,0},{4,5},{5,6},{6,7},{7,4},{8,9},{9,10},{10,1... | collective-permute-start | bytes 9437192 | tf_op jit(solution)/shard_map/ppermute | solution.py:91
  152.2 70.7 %collective-permute-start.2 = (bf16[1024,1536]{1,0:T(8,128)(2,1)}, bf16[1024,1536]{1,0:T(8,128)(2,1)}, u32[]{:S(2)}, u32[]{:S(2)}) collective-permute-start(bf16[1024,1536]{1,0:T(8,128)(2,1)} %collective-permute-done.1), channel_id=1, source_target_pairs={{0,1},{1,2},{2,3},{3,0},{4,5},{5,6},{6,7},{7,4},{8,9},{9,10},{10,1... | collective-permute-start | bytes 9437192 | tf_op jit(solution)/shard_map/ppermute | solution.py:91
  230.4 3.9 copy-start.8
  247.6 3.3 copy-start.6
  269.4 4.5 copy-start.4
  272.0 2.0 copy-start.3
  276.0 176.2 %reduce-scatter.5.cloned.1.call-start = ((), (), s32[]{:S(2)}) async-start(), calls=%async_computation.3 | async-start | bytes 14155776 | tf_op jit(solution)/shard_map/reduce_scatter | solution.py:103
  297.4 314.5 %reduce-scatter.3.cloned.1.call-start = ((), (), s32[]{:S(2)}) async-start(), calls=%async_computation.2 | async-start | bytes 15728640 | tf_op jit(solution)/shard_map/reduce_scatter | solution.py:86
  327.5 18.3 %copy-start.1 = (f32[1024,1024]{1,0:T(8,128)S(1)}, f32[1024,1024]{1,0:T(8,128)}, u32[]{:S(2)}) copy-start(f32[1024,1024]{1,0:T(8,128)} %fusion.20) | copy-start | bytes 12582916
  368.5 19.1 %copy-start.7 = (f32[8,128,128]{2,1,0:T(8,128)S(1)}, f32[8,128,128]{2,1,0:T(8,128)}, u32[]{:S(2)}) copy-start(f32[8,128,128]{2,1,0:T(8,128)} %custom-call.1) | copy-start | bytes 1572868
  368.5 19.1 %copy-start.11 = (bf16[8]{0:T(256)(128)(2,1)S(1)}, bf16[8]{0:T(256)(128)(2,1)}, u32[]{:S(2)}) copy-start(bf16[8]{0:T(256)(128)(2,1)} %get-tuple-element.375) | copy-start | bytes 52
  387.6 31.1 %copy-start.10 = (s32[1024]{0:T(1024)S(1)}, s32[1024]{0:T(1024)}, u32[]{:S(2)}) copy-start(s32[1024]{0:T(1024)} %param.13) | copy-start | bytes 12292
  428.3 2.2 copy-start.2
  428.3 2.9 copy-start.5
Sparse Core Ops, SparseCore 0:
  23.8 28.0 all-gather.6
  276.2 25.5 all-gather.8
  305.3 91.9 reduce-scatter.4
  400.1 211.8 reduce-scatter.2
